TPU v7x, 32 devices: a whole 2x2x4 slice. The times are simulated.
32 devices in a mesh: seq: 16 (over z, y, x), head: 2 (over core).
Axes of the slice: x: 2, y: 2, z: 4, core: 2. Of those that a mesh axis runs over, the one named last changes fastest.
Arguments:
- queries: bfloat16 [2048, 2048], P('seq', 'head'), may hold values from -6 to 6
- key_vectors: bfloat16 [2, 2048, 2048], P(None, 'seq', 'head'), may hold values from -6 to 6
- values: bfloat16 [2, 2048, 2048], P(None, 'seq', 'head'), may hold values from -6 to 6
- strengths: float32 [2, 16, 2048], P(None, 'head', 'seq'), may hold values from 0.05 to 1.95
- out_weight: bfloat16 [2048, 4096], P('head', 'seq'), may hold values from -0.1875 to 0.1875
Outputs:
- mixed: bfloat16 [2048, 4096], P('seq', 'head')
All inputs are finite; a program needn't handle non-finite values.
Results may differ from a plain program's by a relative error of at most 0.014.
Values may be sent and summed in bfloat16 or wider, within the bound.
No kernel may reach another device: no remote copies, remote signals or barrier semaphores. Data moves between devices by JAX's collectives and lax.ppermute only.
A program may use at most 64 MiB of HBM per device.

v0:
```python
import jax
import jax.numpy as jnp
from jax import lax
from jax.sharding import PartitionSpec as P

BLOCK = 64
HIGHEST_PRECISION = lax.Precision.HIGHEST


def carried_in(value, axis, join, neutral):
    count, mine = (lax.axis_size(axis), lax.axis_index(axis))
    pieces = jax.tree.map(lambda part: lax.all_gather(part, axis), value)
    total = jax.tree.map(
        lambda part, zero: jnp.full_like(part, 0) + jnp.asarray(zero, part.dtype), value, neutral
    )

    def hop(position, total):
        longer = join(total, jax.tree.map(lambda part: part[position], pieces))
        return jax.tree.map(lambda new, old: jnp.where(position < mine, new, old), longer, total)

    return lax.fori_loop(0, count - 1, hop, total)


def unit_rows(matrix):
    return matrix * lax.rsqrt(jnp.sum(matrix * matrix, axis=-1, keepdims=True) + 1e-06)


def block_inputs(inputs, first_row):
    queries, key_vectors, values, strengths = inputs
    head_count = strengths.shape[1]
    head_width = queries.shape[1] // head_count
    query_part = (
        lax.dynamic_slice_in_dim(queries, first_row, BLOCK, 0)
        .astype(jnp.float32)
        .reshape(BLOCK, head_count, head_width)
    )
    key_part = (
        lax.dynamic_slice_in_dim(key_vectors, first_row, BLOCK, 1)
        .astype(jnp.float32)
        .reshape(2, BLOCK, head_count, head_width)
    )
    value_part = (
        lax.dynamic_slice_in_dim(values, first_row, BLOCK, 1)
        .astype(jnp.float32)
        .reshape(2, BLOCK, head_count, head_width)
    )
    beta_part = lax.dynamic_slice_in_dim(strengths, first_row, BLOCK, 2)
    query_heads = jnp.transpose(unit_rows(query_part), (1, 0, 2))
    key_heads = jnp.transpose(unit_rows(key_part), (2, 1, 0, 3)).reshape(
        head_count, 2 * BLOCK, head_width
    )
    value_heads = jnp.transpose(value_part, (2, 1, 0, 3)).reshape(head_count, 2 * BLOCK, head_width)
    beta_heads = jnp.transpose(beta_part, (1, 2, 0)).reshape(head_count, 2 * BLOCK)
    return (query_heads, key_heads, value_heads, beta_heads)


def solve_block(key_heads, right_side, beta_heads):
    key_gram = jnp.einsum("hik,hjk->hij", key_heads, key_heads, precision=HIGHEST_PRECISION)
    system = jnp.tril(key_gram, -1) * beta_heads[:, :, None] + jnp.eye(2 * BLOCK, dtype=jnp.float32)
    return jax.scipy.linalg.solve_triangular(
        system, beta_heads[:, :, None] * right_side, lower=True, unit_diagonal=True
    )


def reach_table():
    row_ids = lax.broadcasted_iota(jnp.int32, (BLOCK, 2 * BLOCK), 0)
    col_ids = lax.broadcasted_iota(jnp.int32, (BLOCK, 2 * BLOCK), 1)
    return (col_ids <= 2 * row_ids + 1).astype(jnp.float32)


def compose(earlier, later):
    product = jnp.einsum("hjk,hkl->hjl", earlier[0], later[0], precision=HIGHEST_PRECISION)
    state = jnp.einsum("hjk,hkl->hjl", earlier[1], later[0], precision=HIGHEST_PRECISION) + later[1]
    return (product, state)


def incoming_state(product, local_state, identity_stack, zero_state):
    prefix = carried_in((product, local_state), "seq", compose, (identity_stack, zero_state))
    return prefix[1]


def per_device(queries, key_vectors, values, strengths, out_weight):
    head_count = strengths.shape[1]
    tok_rows = queries.shape[0]
    head_width = queries.shape[1] // head_count
    inputs = (queries, key_vectors, values, strengths)
    first_rows = jnp.arange(tok_rows // BLOCK, dtype=jnp.int32) * BLOCK
    identity_stack = jnp.broadcast_to(
        jnp.eye(head_width, dtype=jnp.float32), (head_count, head_width, head_width)
    )
    zero_state = jnp.zeros((head_count, head_width, head_width), jnp.float32)
    reach_mask = reach_table()

    def ahead_step(carried, first_row):
        local_state, product = carried
        query_heads, key_heads, value_heads, beta_heads = block_inputs(inputs, first_row)
        solved = solve_block(
            key_heads, jnp.concatenate([key_heads, value_heads], axis=2), beta_heads
        )
        key_weights = solved[:, :, :head_width]
        value_weights = solved[:, :, head_width:]
        scores = (
            jnp.einsum("htk,hik->hti", query_heads, key_heads, precision=HIGHEST_PRECISION)
            * reach_mask
        )
        updates = value_weights - jnp.einsum(
            "hik,hvk->hiv", key_weights, local_state, precision=HIGHEST_PRECISION
        )
        out_local = jnp.einsum(
            "hvk,htk->htv", local_state, query_heads, precision=HIGHEST_PRECISION
        ) + jnp.einsum("hti,hiv->htv", scores, updates, precision=HIGHEST_PRECISION)
        reduced = query_heads - jnp.einsum(
            "hti,hik->htk", scores, key_weights, precision=HIGHEST_PRECISION
        )
        lifted = jnp.einsum("htk,hjk->htj", reduced, product, precision=HIGHEST_PRECISION)
        shrink = identity_stack - jnp.einsum(
            "hik,hil->hkl", key_weights, key_heads, precision=HIGHEST_PRECISION
        )
        local_state = local_state + jnp.einsum(
            "hiv,hik->hvk", updates, key_heads, precision=HIGHEST_PRECISION
        )
        product = jnp.einsum("hjk,hkl->hjl", product, shrink, precision=HIGHEST_PRECISION)
        return ((local_state, product), (out_local, lifted))

    (local_state, product), (out_local, lifted) = lax.scan(
        ahead_step, (zero_state, identity_stack), first_rows
    )
    state_in = incoming_state(product, local_state, identity_stack, zero_state)
    heads_out = out_local + jnp.einsum(
        "nhtk,hvk->nhtv", lifted, state_in, precision=HIGHEST_PRECISION
    )
    mixed_heads = (
        jnp.transpose(heads_out, (0, 2, 1, 3))
        .reshape(tok_rows, head_count * head_width)
        .astype(jnp.bfloat16)
    )
    partial_sums = jnp.dot(
        mixed_heads,
        lax.all_gather(out_weight, "seq", axis=1, tiled=True),
        preferred_element_type=jnp.float32,
    )
    return lax.psum_scatter(
        partial_sums.astype(jnp.bfloat16), "head", scatter_dimension=1, tiled=True
    )


def solution(mesh):
    return jax.shard_map(
        per_device,
        mesh=mesh,
        in_specs=(
            P("seq", "head"),
            P(None, "seq", "head"),
            P(None, "seq", "head"),
            P(None, "head", "seq"),
            P("head", "seq"),
        ),
        out_specs=P("seq", "head"),
        check_vma=False,
    )
```

profile of v0, /device:TPU:0, one launch (start us, length us, event | category | flops | bytes accessed | tf_op | source)
XLA Modules:
  0.0 591.6 jit_solution(15922539583316434189)
XLA Ops:
  6.7 200.9 %while.31 = (s32[]{:T(128)}, f32[8,128,128]{2,1,0:T(8,128)S(1)}, f32[8,128,128]{1,2,0:T(8,128)S(1)}, f32[2,8,64,128]{3,2,0,1:T(8,128)}, f32[2,8,64,128]{3,2,0,1:...) while((s32[]{:T(128)}, f32[8,128,128]{2,1,0:T(8,128)S(1)}, ...), condition=%wide.region_3.4_spmd.clone, body=%wide.region_0.3_spmd.clone.sunk | while | flops 1915912320 | bytes 28152272 | solution.py:125
  12.5 1.2 fusion.128
  13.8 79.2 %custom-call.10 = f32[8,1,128,128]{2,3,1,0:T(8,128)} custom-call(f32[8,1,128,128]{3,2,1,0:T(8,128)S(1)} %fusion.128), custom_call_target="InvertDiagBlocksLowerTriangular" | custom-call | tf_op jit(solution)/shard_map/while/body/eval_jaxpr/jit(_solve_triangular)/vmap()/triangular_solve | solution.py:60
  93.6 2.3 fusion.129
  100.7 1.3 fusion.132
  103.6 1.3 fusion.133
  112.9 1.2 fusion.128
  114.1 79.2 %custom-call.10 = f32[8,1,128,128]{2,3,1,0:T(8,128)} custom-call(f32[8,1,128,128]{3,2,1,0:T(8,128)S(1)} %fusion.128), custom_call_target="InvertDiagBlocksLowerTriangular" | custom-call | tf_op jit(solution)/shard_map/while/body/eval_jaxpr/jit(_solve_triangular)/vmap()/triangular_solve | solution.py:60
  193.9 2.3 fusion.129
  201.0 1.3 fusion.132
  204.0 1.3 fusion.133
  210.3 113.6 %all-gather.8.cloned.1.call-done = f32[128,128,128]{2,1,0:T(8,128)} async-done(((f32[8,128,128]{2,1,0:T(8,128)}), f32[128,128,128]{2,1,0:T(8,128)}) %all-gather.8.cloned.1.call-update) | async-done | bytes 8388624 | tf_op jit(solution)/shard_map/all_gather | solution.py:12
  323.9 113.3 %all-gather.10.cloned.1.call-done = f32[128,128,128]{2,1,0:T(8,128)} async-done(((f32[8,128,128]{2,1,0:T(8,128)}), f32[128,128,128]{2,1,0:T(8,128)}) %all-gather.10.cloned.1.call-update) | async-done | bytes 8388624 | tf_op jit(solution)/shard_map/all_gather | solution.py:12
  437.2 51.5 %while.32 = (s32[]{:T(128)}, f32[8,128,128]{1,2,0:T(8,128)S(1)}, s32[]{:T(128)}, f32[16,8,128,128]{3,2,1,0:T(8,128)}, f32[16,8,128,128]{3,2,1,0:T(8,128)}, /*index=5*/s32[]{:T(128)}, s32[]{:T(128)}) while((s32[]{:T(128)}, f32[8,128,128]{1,2,0:T(8,128)S(1)}, s32[]{:T(128)}, f32[16,8,128,128]{3,2,1,0:T(8,128)}, ...), condition=%wide.region_5.6_spmd.clone, body=%wide.region_4.5_spmd.clone.sunk | while | flops 201850880 | bytes 5769315 | solution.py:21
  438.6 2.1 fusion.136
  442.0 2.1 fusion.136
  445.4 2.1 fusion.136
  448.9 2.1 fusion.136
  452.3 2.1 fusion.136
  455.8 2.1 fusion.136
  459.2 2.1 fusion.136
  462.6 2.1 fusion.136
  466.0 2.1 fusion.136
  469.4 2.1 fusion.136
  472.9 2.1 fusion.136
  476.3 2.1 fusion.136
  479.7 2.1 fusion.136
  483.2 2.1 fusion.136
  486.6 2.1 fusion.136
  489.5 83.1 %all-gather.6.cloned.1.call-done = bf16[1024,4096]{1,0:T(8,128)(2,1)} async-done(((bf16[1024,256]{1,0:T(8,128)(2,1)}), bf16[1024,4096]{1,0:T(8,128)(2,1)}) %all-gather.6.cloned.1.call-update) | async-done | bytes 8388624 | tf_op jit(solution)/shard_map/all_gather | solution.py:139
  572.6 5.7 convolution_convert_fusion
  578.3 6.7 %reduce-scatter.2.cloned.1.call-done = bf16[128,2048]{1,0:T(8,128)(2,1)} async-done(((bf16[128,4096]{1,0:T(8,128)(2,1)}), bf16[128,2048]{1,0:T(8,128)(2,1)}) %reduce-scatter.2.cloned.1.call-update) | async-done | bytes 524304 | tf_op jit(solution)/shard_map/reduce_scatter | solution.py:142
  (131 shorter events, 49.1 us)
Async XLA Ops:
  6.5 317.4 %all-gather.8.cloned.1.call-start = ((), (), s32[]{:S(2)}) async-start(), calls=%async_computation.3 | async-start | bytes 8912896 | tf_op jit(solution)/shard_map/all_gather | solution.py:12
  207.6 1.1 copy-start
  208.7 228.5 %all-gather.10.cloned.1.call-start = ((), (), s32[]{:S(2)}) async-start(), calls=%async_computation.4 | async-start | bytes 8912896 | tf_op jit(solution)/shard_map/all_gather | solution.py:12
  209.5 363.1 %all-gather.6.cloned.1.call-start = ((), (), s32[]{:S(2)}) async-start(), calls=%async_computation.1 | async-start | bytes 8912896 | tf_op jit(solution)/shard_map/all_gather | solution.py:139
  210.2 374.8 %reduce-scatter.2.cloned.1.call-start = ((), (), s32[]{:S(2)}) async-start(), calls=%async_computation.2 | async-start | bytes 1572864 | tf_op jit(solution)/shard_map/reduce_scatter | solution.py:142
  437.2 51.5 %copy-start.1 = (f32[2,8,64,128]{3,2,0,1:T(8,128)S(1)}, f32[2,8,64,128]{3,2,0,1:T(8,128)}, u32[]{:S(2)}) copy-start(f32[2,8,64,128]{3,2,0,1:T(8,128)} %get-tuple-element.164) | copy-start | bytes 1572868
  437.2 51.5 %copy-start.2 = (f32[2,8,64,128]{3,2,0,1:T(8,128)S(1)}, f32[2,8,64,128]{3,2,0,1:T(8,128)}, u32[]{:S(2)}) copy-start(f32[2,8,64,128]{3,2,0,1:T(8,128)} %get-tuple-element.168) | copy-start | bytes 1572868
Sparse Core Ops, SparseCore 0:
  208.8 115.0 all-gather.7
  326.7 110.4 all-gather.9
  439.9 132.6 all-gather.5
  578.4 6.5 reduce-scatter.1
where the time goes:
time: 593 us; the launch traced here: 592 us
  waiting for transfers between devices  318 us (54%)
  other arithmetic  164 us (28%)
  matrix products  64 us (11%)
  local copies, waits for them, and re-layouts  26.7 us (5%)
  between operations  13.3 us (2%)
    all_gather x2, waiting for transfers between devices, carried_in(): pieces = jax.tree.map(lambda part: lax.all_gather(part, axis), value)  227 us
    another operation x8, other arithmetic, solve_block(): jax.scipy.linalg.solve_triangular(system, beta_heads[:, :, None] * right_...  159 us
    all_gather x1, waiting for transfers between devices, per_device(): lax.all_gather(out_weight, 'seq', axis=1, tiled=True)  83.1 us
    dot_general x15, matrix products, compose(): jnp.einsum('hjk,hkl->hjl', earlier[1], later[0], precision=HIGHEST_PRECIS...  31 us
    dynamic_slice x30, local copies, waits for them, and re-layouts, hop(): longer = join(total, jax.tree.map(lambda part: part[position], pieces))  19.3 us
  transfers between devices with their start and end apart: 4, of which 4 were waited for; matrix products, arithmetic and copies ran while one was open for 9% of the time, Pallas kernels for 0%

commit v1 on v0

--- a/solution.py
+++ b/solution.py
@@ -136,7 +136,9 @@
     )
     partial_sums = jnp.dot(
         mixed_heads,
-        lax.all_gather(out_weight, "seq", axis=1, tiled=True),
+        jnp.concatenate(
+            lax.all_to_all(jnp.stack([out_weight] * lax.axis_size("seq")), "seq", 0, 0), axis=1
+        ),
         preferred_element_type=jnp.float32,
     )
     return lax.psum_scatter(

time: 593 us -> 662 us (1.12)
  waiting for transfers between devices: 318 us -> 371 us
  starting transfers between devices: 0.12 us -> 8.47 us
    all_gather x2, waiting for transfers between devices: 227 us -> 364 us  [carried_in(): pieces = jax.tree.map(lambda part: lax.all_gather(part, axis), value)]
    all_gather x1 -> x0, waiting for transfers between devices: 83.1 us -> none  [per_device(): lax.all_gather(out_weight, 'seq', axis=1, tiled=True)]
    all_to_all x0 -> x1, starting transfers between devices: none -> 8.39 us  [per_device(): lax.all_to_all(jnp.stack([out_weight] * lax.axis_size('seq')), 'seq', 0, 0)]
  transfers between devices with their start and end apart: 4 -> 4, of which waited for: 4 -> 3; matrix products, arithmetic and copies ran while one was open for 9% -> 9% of each run, Pallas kernels for 0% -> 0%
where the time goes in v1:
time: 662 us; the launch traced here: 660 us
  waiting for transfers between devices  371 us (56%)
  other arithmetic  164 us (25%)
  matrix products  65.6 us (10%)
  local copies, waits for them, and re-layouts  32.1 us (5%)
  between operations  13.3 us (2%)
  starting transfers between devices  8.47 us (1%)
    all_gather x2, waiting for transfers between devices, carried_in(): pieces = jax.tree.map(lambda part: lax.all_gather(part, axis), value)  364 us
    another operation x8, other arithmetic, solve_block(): jax.scipy.linalg.solve_triangular(system, beta_heads[:, :, None] * right_...  159 us
    dot_general x15, matrix products, compose(): jnp.einsum('hjk,hkl->hjl', earlier[1], later[0], precision=HIGHEST_PRECIS...  30.9 us
    dynamic_slice x30, local copies, waits for them, and re-layouts, hop(): longer = join(total, jax.tree.map(lambda part: part[position], pieces))  19.2 us
  transfers between devices with their start and end apart: 4, of which 3 were waited for; matrix products, arithmetic and copies ran while one was open for 9% of the time, Pallas kernels for 0%

profile of v1, /device:TPU:0, one launch (start us, length us, event | category | flops | bytes accessed | tf_op | source)
XLA Modules:
  0.0 660.3 jit_solution(17176737119712990820)
XLA Ops:
  6.7 200.9 %while.31 = (s32[]{:T(128)}, f32[8,128,128]{2,1,0:T(8,128)S(1)}, f32[8,128,128]{1,2,0:T(8,128)S(1)}, f32[2,8,64,128]{3,2,0,1:T(8,128)}, f32[2,8,64,128]{3,2,0,1:...) while((s32[]{:T(128)}, f32[8,128,128]{2,1,0:T(8,128)S(1)}, ...), condition=%wide.region_3.4_spmd.clone, body=%wide.region_0.3_spmd.clone.sunk | while | flops 1915912320 | bytes 28152272 | solution.py:125
  13.8 79.2 %custom-call.10 = f32[8,1,128,128]{2,3,1,0:T(8,128)} custom-call(f32[8,1,128,128]{3,2,1,0:T(8,128)S(1)} %fusion.128), custom_call_target="InvertDiagBlocksLowerTriangular" | custom-call | tf_op jit(solution)/shard_map/while/body/eval_jaxpr/jit(_solve_triangular)/vmap()/triangular_solve | solution.py:60
  93.6 2.3 fusion.129
  100.7 1.3 fusion.132
  103.6 1.3 fusion.133
  114.1 79.2 %custom-call.10 = f32[8,1,128,128]{2,3,1,0:T(8,128)} custom-call(f32[8,1,128,128]{3,2,1,0:T(8,128)S(1)} %fusion.128), custom_call_target="InvertDiagBlocksLowerTriangular" | custom-call | tf_op jit(solution)/shard_map/while/body/eval_jaxpr/jit(_solve_triangular)/vmap()/triangular_solve | solution.py:60
  193.9 2.3 fusion.129
  201.0 1.3 fusion.132
  204.0 1.4 fusion.133
  209.5 1.2 copy.104
  210.8 4.3 stack.2
  215.1 8.4 %all-to-all-start = ((bf16[16,1024,256]{1,2,0:T(8,128)(2,1)}), bf16[16,1024,256]{1,2,0:T(8,128)(2,1)}, u32[]{:S(2)}, u32[]{:S(2)}) async-start(bf16[16,1024,256]{1,2,0:T(8,128)(2,1)} %stack.2), calls=%async_computation | async-start | bytes 16777216 | tf_op jit(solution)/shard_map/all_to_all | solution.py:140
  223.5 242.1 %all-gather.5.cloned.1.call-done = f32[128,128,128]{2,1,0:T(8,128)} async-done(((f32[8,128,128]{2,1,0:T(8,128)}), f32[128,128,128]{2,1,0:T(8,128)}) %all-gather.5.cloned.1.call-update) | async-done | bytes 8388624 | tf_op jit(solution)/shard_map/all_gather | solution.py:12
  465.6 121.8 %all-gather.7.cloned.1.call-done = f32[128,128,128]{2,1,0:T(8,128)} async-done(((f32[8,128,128]{2,1,0:T(8,128)}), f32[128,128,128]{2,1,0:T(8,128)}) %all-gather.7.cloned.1.call-update) | async-done | bytes 8388624 | tf_op jit(solution)/shard_map/all_gather | solution.py:12
  587.4 51.4 %while.32 = (s32[]{:T(128)}, f32[8,128,128]{1,2,0:T(8,128)S(1)}, s32[]{:T(128)}, f32[16,8,128,128]{3,2,1,0:T(8,128)}, f32[16,8,128,128]{3,2,1,0:T(8,128)}, /*index=5*/s32[]{:T(128)}, s32[]{:T(128)}) while((s32[]{:T(128)}, f32[8,128,128]{1,2,0:T(8,128)S(1)}, s32[]{:T(128)}, f32[16,8,128,128]{3,2,1,0:T(8,128)}, ...), condition=%wide.region_5.6_spmd.clone, body=%wide.region_4.5_spmd.clone.sunk | while | flops 201850880 | bytes 5769315 | solution.py:21
  588.9 2.1 fusion.136
  592.3 2.1 fusion.136
  595.7 2.1 fusion.136
  599.1 2.1 fusion.136
  602.5 2.1 fusion.136
  606.0 2.1 fusion.136
  609.4 2.1 fusion.136
  612.8 2.1 fusion.136
  616.2 2.1 fusion.136
  619.6 2.1 fusion.136
  623.1 2.1 fusion.136
  626.5 2.1 fusion.136
  629.9 2.1 fusion.136
  633.3 2.1 fusion.136
  636.8 2.1 fusion.136
  639.7 7.3 %convolution_convert_fusion = bf16[128,4096]{1,0:T(8,128)(2,1)} fusion(bf16[1024,4096]{0,1:T(8,128)(2,1)} %bitcast.6, bf16[16,8,8,128]{3,2,1,0:T(8,128)(2,1)S(1)} %bitcast.211), kind=kOutput, calls=%fused_computation.74 | convolution fusion | flops 1074266112 | bytes 9699328 | tf_op jit(solution)/shard_map/dot_general | solution.py:137
  647.0 6.7 %reduce-scatter.2.cloned.1.call-done = bf16[128,2048]{1,0:T(8,128)(2,1)} async-done(((bf16[128,4096]{1,0:T(8,128)(2,1)}), bf16[128,2048]{1,0:T(8,128)(2,1)}) %reduce-scatter.2.cloned.1.call-update) | async-done | bytes 524304 | tf_op jit(solution)/shard_map/reduce_scatter | solution.py:144
  (132 shorter events, 50.8 us)
Async XLA Ops:
  6.5 459.1 %all-gather.5.cloned.1.call-start = ((), (), s32[]{:S(2)}) async-start(), calls=%async_computation.3 | async-start | bytes 8912896 | tf_op jit(solution)/shard_map/all_gather | solution.py:12
  207.7 1.1 copy-start
  208.8 378.7 %all-gather.7.cloned.1.call-start = ((), (), s32[]{:S(2)}) async-start(), calls=%async_computation.4 | async-start | bytes 8912896 | tf_op jit(solution)/shard_map/all_gather | solution.py:12
  215.1 424.6 %all-to-all-start = ((bf16[16,1024,256]{1,2,0:T(8,128)(2,1)}), bf16[16,1024,256]{1,2,0:T(8,128)(2,1)}, u32[]{:S(2)}, u32[]{:S(2)}) async-start(bf16[16,1024,256]{1,2,0:T(8,128)(2,1)} %stack.2), calls=%async_computation | async-start | bytes 16777216 | tf_op jit(solution)/shard_map/all_to_all | solution.py:140
  223.5 430.3 %reduce-scatter.2.cloned.1.call-start = ((), (), s32[]{:S(2)}) async-start(), calls=%async_computation.2 | async-start | bytes 1572864 | tf_op jit(solution)/shard_map/reduce_scatter | solution.py:144
  587.4 51.4 %copy-start.1 = (f32[2,8,64,128]{3,2,0,1:T(8,128)S(1)}, f32[2,8,64,128]{3,2,0,1:T(8,128)}, u32[]{:S(2)}) copy-start(f32[2,8,64,128]{3,2,0,1:T(8,128)} %get-tuple-element.164) | copy-start | bytes 1572868
  587.4 51.4 %copy-start.2 = (f32[2,8,64,128]{3,2,0,1:T(8,128)S(1)}, f32[2,8,64,128]{3,2,0,1:T(8,128)}, u32[]{:S(2)}) copy-start(f32[2,8,64,128]{3,2,0,1:T(8,128)} %get-tuple-element.168) | copy-start | bytes 1572868
Sparse Core Ops, SparseCore 0:
  208.9 256.6 all-gather.4
  468.4 119.0 all-gather.6
  647.2 6.5 reduce-scatter.1
